TPU v7x, 16 devices: a whole 2x2x2 slice. The times are simulated.
16 devices in a mesh: ep: 16 (over z, y, x, core).
Axes of the slice: x: 2, y: 2, z: 2, core: 2. Of those that a mesh axis runs over, the one named last changes fastest.
Arguments:
- x: bfloat16 [4096, 2048], P('ep')
- gate_w: bfloat16 [2048, 64], replicated
- up_w: bfloat16 [64, 2048, 1408], P('ep')
- down_w: bfloat16 [64, 1408, 2048], P('ep')
- expert_picks: int32 [64, 128], P('ep')
- loss_w: bfloat16 [4096, 2048], P('ep')
Outputs:
- output 1: bfloat16 [4096, 2048], P('ep')
- output 2: float32 [], replicated
- output 3: bfloat16 [4096, 2048], P('ep')
- output 4: bfloat16 [64, 2048, 1408], P('ep')
- output 5: bfloat16 [64, 1408, 2048], P('ep')
- output 6: float32 [2048, 64], replicated
All inputs are finite; a program needn't handle non-finite values.
Results may differ from a plain program's by a relative error of at most 0.02.
Values are sent between devices in bfloat16 or wider.
A program may use at most 1 GiB of HBM per device.

v0:
```python
import functools
import math
import jax
import jax.numpy as jnp
from jax import lax
from jax.experimental import pallas as pl
from jax.experimental.pallas import tpu as pltpu
from jax.sharding import PartitionSpec as P

BF = jnp.bfloat16
F32 = jnp.float32
MESH = pl.DeviceIdType.MESH
N = 16
TOK = 256
LE = 4
CAP = 128
HID = 2048
FF = 1408
CH = 512
NCH = HID // CH
FIRST = 4
HALF = HID // 2
NOW = 2
ORDER = (14, 15, 6, 10, 12, 7, 11, 13, 2, 4, 8, 3, 5, 9, 1)


def dot(a, b, ca=1, cb=0):
    return lax.dot_general(a, b, (((ca,), (cb,)), ((), ())), preferred_element_type=F32)


def iota(shape, dim):
    return lax.broadcasted_iota(jnp.int32, shape, dim)


def ones_where(cond):
    return jnp.where(cond, 1.0, 0.0).astype(BF)


def split3(v):
    hi = v.astype(BF)
    rest = v - hi.astype(F32)
    mid = rest.astype(BF)
    low = (rest - mid.astype(F32)).astype(BF)
    return hi, mid, low


def flip(me, k):
    out = 0
    for b in range(4):
        bit = (me // (1 << b)) % 2
        if (k >> b) & 1:
            bit = 1 - bit
        out = out + bit * (1 << b)
    return out


def comm_kernel(scale, sel_ref, x_hbm, gw_hbm, up_hbm, dn_hbm, r_hbm,
                y_out, gnow_out, glater_out, tab_out, gg_out, loss_out, xl_out, u_out, dh_out, da_out,
                x_v, r_v, gw_v, w1, w2, xsend, rsend, xrecv, rrecv, hsend, hrecv, gsend,
                xl_v, dh_v, u_v, gp_v, da_v, ggpart, ggpair, gghalf, ggrecv, ggall, selsend, selall, gates, gates_all,
                losssend, lossall, dgsend, dgall, one_v, c_v, e_v, probs_v, dlog_v,
                ld_sem, w_sem, out_sem, send_sem, recv_sem):
    me = lax.axis_index('ep')
    peers = [flip(me, k) for k in ORDER]
    core, chip, twin = me % 2, me // 2, flip(me, 1)
    others = [flip(me, k) for k in ORDER if k % 2 == 0]

    def load(src, dst, i):
        return pltpu.make_async_copy(src, dst, ld_sem.at[i])

    def weight1(e, slot):
        return pltpu.make_async_copy(up_hbm.at[e], w1.at[slot], w_sem.at[0, slot])

    def weight2(e, slot):
        return pltpu.make_async_copy(dn_hbm.at[e], w2.at[slot], w_sem.at[1, slot])

    def push(src, dst, peer, i):
        return pltpu.make_async_remote_copy(src_ref=src, dst_ref=dst, send_sem=send_sem.at[0 if i == 1 else 1], recv_sem=recv_sem.at[i],
                                            device_id=(peer,), device_id_type=MESH)

    def wait_recv(buf, i, n=N - 1):
        part = buf.at[pl.ds(0, n)]
        pltpu.make_async_copy(part, part, recv_sem.at[i]).wait()

    def wait_send(buf, i, n=N - 1):
        part = buf.at[pl.ds(0, n)]
        pltpu.make_async_copy(part, part, send_sem.at[0 if i == 1 else 1]).wait()

    cp_x = load(x_hbm, x_v, 0)
    cp_g = load(gw_hbm, gw_v, 0)
    cp_r = load(r_hbm, r_v, 1)
    cp_x.start()
    cp_g.start()
    cp_r.start()

    sel = sel_ref[...]
    selsend[...] = jnp.zeros_like(selsend)
    selsend[0:LE, :] = sel
    selall[pl.ds(me, 1)] = selsend[...].reshape(1, 8, CAP)

    barrier = pltpu.get_barrier_semaphore()
    for p in peers:
        pl.semaphore_signal(barrier, inc=1, device_id=(p,), device_id_type=MESH)
    pl.semaphore_wait(barrier, N - 1)

    for p in peers:
        push(selsend, selall.at[me], p, 0).start()
    for e in range(3):
        weight1(e, e).start()
        weight2(e, e).start()

    cp_g.wait()
    cp_x.wait()
    logits = dot(x_v[...], gw_v[...], 1, 1)
    ex = jnp.exp(logits - jnp.max(logits, axis=1, keepdims=True))
    probs = ex / jnp.sum(ex, axis=1, keepdims=True)
    probs_v[...] = probs

    below = ones_where(iota((TOK, TOK), 1) < iota((TOK, TOK), 0))
    slot_lane = (iota((TOK, TOK), 1) % 16).astype(F32)

    tok_row = iota((TOK, CAP), 0)
    same = iota((CAP, TOK), 0) // 8 == iota((CAP, TOK), 1) // 16
    fold = ones_where(same)
    base = (iota((1, CAP), 1) // 8) * TOK
    hits = [ones_where(tok_row == sel[l:l + 1, :] - base) for l in range(LE)]
    count = dot(hits[0], fold)
    for l in range(1, LE):
        count = count + dot(hits[l], fold)
    pres = count > 0.5
    rank = dot(below, ones_where(pres))
    pick_of = jnp.where(pres, jnp.where(rank == slot_lane, 1.0, 0.0), 0.0).astype(BF)
    for l in range(LE):
        e_v[l] = jnp.where(same, dot(hits[l], pick_of, 0, 0), 0.0).astype(BF)

    place = ones_where(iota((CAP, 512), 0) % 8 == iota((CAP, 512), 1) % 8)
    fold2 = ones_where((iota((512, TOK), 0) % 256) // 16 == iota((512, TOK), 1) // 16)
    for_wait = selall.at[pl.ds(0, N - 1)]
    pltpu.make_async_copy(for_wait, for_wait, recv_sem.at[0]).wait()
    everyone = selall[...].reshape(8 * N, CAP)
    mine = jnp.where(iota((8 * N, CAP), 1) // 8 == me, everyone - me * TOK, 0).astype(F32).astype(BF)
    spread = dot(mine, place)
    lane = iota((8 * N, 512), 1)
    want = ((lane % 256) // 16) * 8 + 2 * (lane // 256) + (lane % 16) // 8
    ids = jnp.sum(jnp.where(iota((8 * N, 512), 0) == want, spread, 0.0), axis=0, keepdims=True)
    one = jnp.where(iota((TOK, 512), 0).astype(F32) == ids, 1.0, 0.0)
    one_v[...] = one.astype(BF)
    pres2 = dot(one_v[...], fold2) > 0.5
    rank2 = dot(below, ones_where(pres2))
    give = jnp.where(pres2, jnp.where(rank2 == slot_lane, 1.0, 0.0), 0.0).astype(BF)
    give_t = give.T

    def gather(src, dst):
        def step(c, carry):
            cols = pl.ds(pl.multiple_of(c * CH, CH), CH)
            dst[:, :, cols] = dot(give_t, src[:, cols]).astype(BF).reshape(N, 16, CH)
            return carry
        lax.fori_loop(0, NCH, step, 0)

    for c in range(NCH):
        cols = pl.ds(c * CH, CH)
        xsend[:, :, cols] = dot(give_t, x_v[:, cols]).astype(BF).reshape(N, 16, CH)
        for p in peers:
            push(xsend.at[p, :, cols], xrecv.at[me, :, cols], p, 1).start()
    xrecv[pl.ds(me, 1)] = xsend[pl.ds(me, 1)]

    rep = ones_where(iota((64, 512), 0) == 4 * ((iota((64, 512), 1) % 256) // 16) + 2 * (iota((64, 512), 1) // 256)
                     + (iota((64, 512), 1) % 16) // 8)
    wide = 0.0
    for term in split3(probs_v[...]):
        wide = wide + dot(term, rep)
    comb = wide * one
    for i, term in enumerate(split3(comb)):
        c_v[i] = term
    gates[...] = jnp.sum(comb, axis=0, keepdims=True)
    for p in peers:
        push(gates, gates_all.at[me], p, 2).start()
    gates_all[pl.ds(me, 1)] = gates[...].reshape(1, 1, 512)

    cp_r.wait()
    gather(r_v, rsend)
    for p in peers:
        push(rsend.at[p], rrecv.at[me], p, 3).start()
    rrecv[pl.ds(me, 1)] = rsend[pl.ds(me, 1)]

    wait_recv(xrecv, 1)

    def send_h(q, start, width):
        cols = pl.ds(start, width)
        for p in peers:
            push(hsend.at[q, p, :, cols], hrecv.at[q, me, :, cols], p, 4).start()

    def wait_h(buf, sem):
        part = buf.at[:, pl.ds(0, N - 1)]
        pltpu.make_async_copy(part, part, sem).wait()

    def fwd(q, carry):
        for j in range(2):
            e = 2 * q + j
            slot = e % 3
            xl = dot(e_v[e], xrecv[...].reshape(TOK, HID)).astype(BF)
            xl_v[e] = xl
            weight1(e, slot).wait()
            a = dot(xl_v[e], w1[slot])
            if j == 0:
                @pl.when(q == 0)
                def _():
                    weight1(3, 0).start()
            k0 = math.sqrt(2.0 / math.pi)
            t = jnp.tanh(k0 * (a + 0.044715 * (a * a * a)))
            u_v[e] = (0.5 * a * (1.0 + t)).astype(BF)
            gp_v[e] = 0.5 * (1.0 + t) + 0.5 * a * (1.0 - t * t) * (k0 * (1.0 + 3.0 * 0.044715 * (a * a)))
        weight2(2 * q, (2 * q) % 3).wait()
        weight2(2 * q + 1, (2 * q + 1) % 3).wait()

        def step(c, carry):
            cols = pl.ds(pl.multiple_of(c * CH, CH), CH)
            outs = [dot(u_v[2 * q + j], w2[(2 * q + j) % 3, :, cols]).reshape(N, 8, CH) for j in range(2)]
            hsend[q, :, :, cols] = jnp.concatenate(outs, axis=1).astype(BF)
            return carry
        lax.fori_loop(0, NCH, step, 0)

        @pl.when(q == 0)
        def _():
            weight2(3, 0).start()
        hrecv[q, pl.ds(me, 1)] = hsend[q, pl.ds(me, 1)]

        @pl.when(q == 0)
        def _():
            send_h(0, 0, HALF)
        return carry
    lax.fori_loop(0, 2, fwd, 0)
    pltpu.make_async_copy(xl_v, xl_out, out_sem.at[0]).start()
    pltpu.make_async_copy(u_v, u_out, out_sem.at[0]).start()

    wait_recv(gates_all, 2)
    wait_recv(rrecv, 3)

    def send_now(c):
        cols = pl.ds(c * CH, CH)
        for p in peers:
            push(gsend.at[1, p, :, cols], gnow_out.at[me, :, cols], p, 5).start()
        pltpu.make_async_copy(gsend.at[1, me, :, cols], gnow_out.at[me, :, cols], out_sem.at[0]).start()

    lane128 = iota((CAP, 128), 1)
    rows = jnp.broadcast_to(gates_all[...], (N, 8, 512)).reshape(CAP, 512)

    def pre(q, table):
        gcol = []
        for j in range(2):
            here = iota((CAP, 512), 1) == q * 256 + me * 16 + j * 8 + iota((CAP, 512), 0) % 8
            gcol.append(jnp.sum(jnp.where(here, rows, 0.0), axis=1, keepdims=True))

        def rstep(c, acc):
            cols = pl.ds(pl.multiple_of(c * CH, CH), CH)
            rall = rrecv[:, :, cols].reshape(TOK, CH)
            hall = hsend[q, :, :, cols].astype(F32)
            out = []
            for j in range(2):
                rl = dot(e_v[2 * q + j], rall)
                dh_v[2 * q + j, :, cols] = (gcol[j] * (rl * scale)).astype(BF)
                prod = rl * hall[:, 8 * j:8 * j + 8, :].reshape(CAP, CH)
                out.append(acc[j] + ((prod[:, 0:128] + prod[:, 128:256]) + (prod[:, 256:384] + prod[:, 384:512])))
            return tuple(out)
        zero = jnp.zeros((CAP, 128), F32)
        acc = lax.fori_loop(0, NCH, rstep, (zero, zero))
        for j in range(2):
            table = table + jnp.where(lane128 == 2 * q + j, jnp.sum(acc[j], axis=1, keepdims=True) * scale, 0.0)
        return table
    dgsend[...] = lax.fori_loop(0, 2, pre, jnp.zeros((CAP, 128), F32)).reshape(N, 8, 128)
    for p in peers:
        push(dgsend.at[p], dgall.at[me], p, 6).start()
    dgall[pl.ds(me, 1)] = dgsend[pl.ds(me, 1)]
    send_h(0, HALF, HALF)
    send_h(1, 0, HALF)

    def gate_grads():
        wait_recv(dgall, 6)
        mine_of = []
        for l in range(LE):
            col = jnp.sum(jnp.where(iota((N, 8, 128), 2) == l, dgall[...], 0.0), axis=2, keepdims=True).reshape(CAP, 1)
            mine_of.append(jnp.where(iota((CAP, 64), 1) == 4 * (iota((CAP, 64), 0) // 8) + l, col, 0.0).reshape(N, 8, 64))
        spread_g = jnp.concatenate([jnp.concatenate(mine_of[2 * q:2 * q + 2], axis=1).reshape(256, 64) for q in range(2)], axis=0)
        ds = 0.0
        for term in split3(spread_g):
            ds = ds + dot(one_v[...], term)
        probs = probs_v[...]
        dlog = (probs * (ds - jnp.sum(probs * ds, axis=1, keepdims=True))).astype(BF)
        dlog_v[...] = jnp.concatenate([dlog, jnp.zeros_like(dlog)], axis=1)
        dlog_t = dlog.astype(F32).T.astype(BF)
        for c in range(NCH):
            part = dot(dlog_t, x_v[:, c * CH:(c + 1) * CH])
            for i in range(CH // 128):
                ggpart[c // 2, (c % 2) * (CH // 128) + i] = part[:, i * 128:(i + 1) * 128]
        push(ggpart.at[1 - core], ggpair, twin, 8).start()

    def gate_scatter():
        push(ggpart.at[1 - core], ggpair, twin, 8).wait_recv()
        gghalf[...] = ggpart[core] + ggpair[...]
        for p in others:
            push(gghalf.at[p // 2], ggrecv.at[chip], p, 9).start()
        ggrecv[pl.ds(chip, 1)] = gghalf[pl.ds(chip, 1)]
        send_h(1, HALF + CH, CH)
        send_now(0)

    def gate_gather():
        wait_recv(ggrecv, 9, 7)
        total = ggrecv[0]
        for i in range(1, 8):
            total = total + ggrecv[i]
        ggall[core, pl.ds(chip, 1)] = total.reshape(1, 64, 128)
        for p in others:
            push(ggall.at[core, chip], ggall.at[core, chip], p, 10).start()
        for c in range(1, NOW):
            send_now(c)

    def bwd(q, carry):
        for j in range(2):
            e = (1 - q) * (2 + j) + q * (1 - j)
            slot = (1 - q) * (2 - 2 * j) + q * (1 + j)
            if j == 1:
                @pl.when(q == 1)
                def _():
                    weight2(0, 2).wait()
            du = dot(dh_v[e], w2[slot], 1, 1).astype(BF).astype(F32)
            da_v[e] = (gp_v[e] * du).astype(BF)
            if j == 0:
                @pl.when(q == 0)
                def _():
                    weight2(0, 2).start()

        @pl.when(q == 1)
        def _():
            gate_scatter()
            weight1(0, 2).wait()

        def step(c, carry):
            cols = pl.ds(pl.multiple_of(c * CH, CH), CH)
            outs = []
            for j in range(2):
                slot = (1 - q) * (2 - 2 * j) + q * (2 - j)
                outs.append(dot(da_v[2 * (1 - q) + j], w1[slot, cols, :], 1, 1).reshape(N, 8, CH))
            gsend[1 - q, :, :, cols] = jnp.concatenate(outs, axis=1).astype(BF)
            return carry
        lax.fori_loop(0, NCH, step, 0)

        @pl.when(q == 0)
        def _():
            weight1(0, 2).start()
            gate_grads()
            send_h(1, HALF, CH)
        return carry
    lax.fori_loop(0, 2, bwd, 0)
    later = [pltpu.make_async_copy(gsend.at[0], glater_out.at[:, :, pl.ds(0, HID)], out_sem.at[0])]
    if NOW < NCH:
        later.append(pltpu.make_async_copy(gsend.at[1, :, :, pl.ds(NOW * CH, HID - NOW * CH)],
                                           glater_out.at[:, :, pl.ds(HID, HID - NOW * CH)], out_sem.at[0]))
    for cp in later:
        cp.start()
    pltpu.make_async_copy(dh_v, dh_out, out_sem.at[0]).start()
    pltpu.make_async_copy(da_v, da_out, out_sem.at[0]).start()

    cp_dlog = pltpu.make_async_copy(dlog_v, tab_out.at[:, pl.ds(512, 128)], out_sem.at[0])
    cp_dlog.start()
    cp_one = pltpu.make_async_copy(one_v, tab_out.at[:, pl.ds(0, 512)], out_sem.at[0])
    cp_one.start()

    gate_gather()

    wait_h(hrecv, recv_sem.at[4])
    wait_send(xsend, 1)

    def ystep(c, acc):
        cols = pl.ds(pl.multiple_of(c * CH, CH), CH)
        h = hrecv[:, :, :, cols].reshape(512, CH)
        tot = x_v[:, cols].astype(F32) + (dot(c_v[0], h) + dot(c_v[1], h) + dot(c_v[2], h))
        y = tot.astype(BF)
        xsend[:, :, cols] = y.reshape(N, 16, CH)
        return acc + jnp.sum(y.astype(F32) * r_v[:, cols].astype(F32), axis=0, keepdims=True)
    losssend[...] = lax.fori_loop(0, NCH, ystep, jnp.zeros((1, CH), F32))
    cp_y = pltpu.make_async_copy(xsend, y_out, out_sem.at[0])
    cp_y.start()
    for p in peers:
        push(losssend, lossall.at[me], p, 7).start()
    lossall[pl.ds(me, 1)] = losssend[...].reshape(1, 1, CH)

    wait_recv(ggall.at[core], 10, 7)
    across = push(ggall.at[core], ggall.at[core], twin, 11)
    across.start()
    across.wait_recv()
    cp_gg = [pltpu.make_async_copy(ggall.at[i // 8, i % 8], gg_out.at[:, pl.ds(i * 128, 128)], out_sem.at[0]) for i in range(N)]
    for cp in cp_gg:
        cp.start()
    wait_recv(lossall, 7)
    loss_out[0, 0] = jnp.sum(lossall[...]) * scale
    wait_recv(gnow_out, 5)

    wait_send(selall, 0)
    wait_send(gates_all, 2)
    wait_h(hsend, send_sem.at[1])
    wait_send(dgall, 6)
    part = gsend.at[1, pl.ds(0, N - 1), :, pl.ds(0, NOW * CH)]
    pltpu.make_async_copy(part, part, send_sem.at[1]).wait()
    for c in range(NOW):
        cols = pl.ds(c * CH, CH)
        pltpu.make_async_copy(gsend.at[1, me, :, cols], gnow_out.at[me, :, cols], out_sem.at[0]).wait()
    wait_send(rsend, 3)
    wait_send(lossall, 7)
    push(ggpart.at[1 - core], ggpair, twin, 8).wait_send()
    wait_send(gghalf, 9, 7)
    wait_send(ggall.at[core], 10, 7)
    across.wait_send()
    for cp in later:
        cp.wait()
    cp_dlog.wait()
    cp_one.wait()
    pltpu.make_async_copy(xl_v, xl_out, out_sem.at[0]).wait()
    pltpu.make_async_copy(u_v, u_out, out_sem.at[0]).wait()
    pltpu.make_async_copy(dh_v, dh_out, out_sem.at[0]).wait()
    pltpu.make_async_copy(da_v, da_out, out_sem.at[0]).wait()
    cp_y.wait()
    for cp in cp_gg:
        cp.wait()


def comm_call(sel, x, gw, up, dn, r, scale):
    any_ = pl.BlockSpec(memory_space=pl.ANY)
    vmem = pl.BlockSpec(memory_space=pltpu.VMEM)
    V = pltpu.VMEM
    shape = jax.ShapeDtypeStruct
    return pl.pallas_call(
        functools.partial(comm_kernel, scale),
        out_shape=[shape((N, 16, HID), BF), shape((N, 16, NOW * CH), BF), shape((N, 16, 2 * HID - NOW * CH), BF), shape((TOK, 640), BF),
                   shape((64, HID), F32), shape((1, 1), F32),
                   shape((LE, CAP, HID), BF), shape((LE, CAP, FF), BF), shape((LE, CAP, HID), BF), shape((LE, CAP, FF), BF)],
        in_specs=[vmem, any_, any_, any_, any_, any_],
        out_specs=[any_, any_, any_, any_, any_, pl.BlockSpec(memory_space=pltpu.SMEM), any_, any_, any_, any_],
        scratch_shapes=[
            V((TOK, HID), BF), V((TOK, HID), BF), V((64, HID), BF),
            V((3, HID, FF), BF), V((3, FF, HID), BF),
            V((N, 16, HID), BF), V((N, 16, HID), BF), V((N, 16, HID), BF), V((N, 16, HID), BF),
            V((2, N, 16, HID), BF), V((2, N, 16, HID), BF), V((2, N, 16, HID), BF),
            V((LE, CAP, HID), BF), V((LE, CAP, HID), BF), V((LE, CAP, FF), BF), V((LE, CAP, FF), F32), V((LE, CAP, FF), BF),
            V((2, 8, 64, 128), F32), V((8, 64, 128), F32), V((8, 64, 128), F32), V((8, 64, 128), F32), V((2, 8, 64, 128), F32),
            V((8, CAP), jnp.int32), V((N, 8, CAP), jnp.int32), V((1, 512), F32), V((N, 1, 512), F32),
            V((1, CH), F32), V((N, 1, CH), F32), V((N, 8, 128), F32), V((N, 8, 128), F32),
            V((TOK, 512), BF), V((3, TOK, 512), BF), V((LE, CAP, TOK), BF), V((TOK, 64), F32), V((TOK, 128), BF),
            pltpu.SemaphoreType.DMA((2,)), pltpu.SemaphoreType.DMA((2, 3)), pltpu.SemaphoreType.DMA((1,)),
            pltpu.SemaphoreType.DMA((2,)), pltpu.SemaphoreType.DMA((12,)),
        ],
        compiler_params=pltpu.CompilerParams(collective_id=0, has_side_effects=True, vmem_limit_bytes=67043328),
        name='exchange',
    )(sel, x, gw, up, dn, r)


def tile_tools(ins, bufs, outs, tiles, in_sem, out_sem, first):
    def loads(e):
        return [pltpu.make_async_copy(src.at[e], dst.at[e - first], in_sem.at[e - first]) for src, dst in zip(ins, bufs)]

    def stores(i):
        e, c = i // NCH, i % NCH
        cols = pl.ds(pl.multiple_of(c * CH, CH), CH)
        return [pltpu.make_async_copy(tiles[0].at[i - first * NCH], outs[0].at[e, cols, :], out_sem.at[0]),
                pltpu.make_async_copy(tiles[1].at[i - first * NCH], outs[1].at[e, :, cols], out_sem.at[1])]

    def step(i, carry):
        e, c = i // NCH, i % NCH
        xl_v, da_v, u_v, dh_v = bufs
        cols = pl.ds(pl.multiple_of(c * CH, CH), CH)
        tiles[0][i - first * NCH] = dot(xl_v[e - first, :, cols], da_v[e - first], 0, 0).astype(BF)
        tiles[1][i - first * NCH] = dot(u_v[e - first], dh_v[e - first, :, cols], 0, 0).astype(BF)
        for cp in stores(i):
            cp.start()
        return carry

    def finish(i, carry):
        for cp in stores(i):
            cp.wait()
        return carry
    return loads, step, finish


def wgrad1_kernel(xl_in, da_in, u_in, dh_in, y_in, gg_in, loss_in, g1, g2, y, gg, loss,
                  xl_v, da_v, u_v, dh_v, y_v, gg_v, t1, t2, in_sem, out_sem):
    loads, step, finish = tile_tools((xl_in, da_in, u_in, dh_in), (xl_v, da_v, u_v, dh_v), (g1, g2), (t1, t2), in_sem, out_sem, 0)
    cp_y = pltpu.make_async_copy(y_in, y_v, in_sem.at[LE])
    cp_gg = pltpu.make_async_copy(gg_in, gg_v, in_sem.at[LE + 1])
    for cp in loads(0):
        cp.start()
    loss[0, 0] = loss_in[0, 0]

    def expert(e, carry):
        for cp in loads(e):
            cp.wait()

        @pl.when(e + 1 < FIRST)
        def _():
            for cp in loads(e + 1):
                cp.start()

        @pl.when(e == 0)
        def _():
            cp_y.start()
            cp_gg.start()
        lax.fori_loop(e * NCH, (e + 1) * NCH, step, 0)
        return carry
    lax.fori_loop(0, FIRST, expert, 0)
    cp_y.wait()
    cp_gg.wait()
    out_y = pltpu.make_async_copy(y_v, y, in_sem.at[LE])
    out_gg = pltpu.make_async_copy(gg_v, gg, in_sem.at[LE + 1])
    out_y.start()
    out_gg.start()
    out_y.wait()
    out_gg.wait()
    lax.fori_loop(0, FIRST * NCH, finish, 0)


def wgrad1_call(xl, da, u, dh, y, gg, loss):
    shape = jax.ShapeDtypeStruct
    any_ = pl.BlockSpec(memory_space=pl.ANY)
    smem = pl.BlockSpec(memory_space=pltpu.SMEM)
    V = pltpu.VMEM
    return pl.pallas_call(
        wgrad1_kernel,
        in_specs=[any_] * 6 + [smem],
        out_specs=[any_] * 4 + [smem],
        out_shape=[shape((LE, HID, FF), BF), shape((LE, FF, HID), BF), shape((N, 16, HID), BF), shape((64, HID), F32), shape((1, 1), F32)],
        scratch_shapes=[V((FIRST, CAP, HID), BF), V((FIRST, CAP, FF), BF), V((FIRST, CAP, FF), BF), V((FIRST, CAP, HID), BF),
                        V((N, 16, HID), BF), V((64, HID), F32), V((FIRST * NCH, CH, FF), BF), V((FIRST * NCH, FF, CH), BF),
                        pltpu.SemaphoreType.DMA((LE + 2,)), pltpu.SemaphoreType.DMA((2,))],
        compiler_params=pltpu.CompilerParams(vmem_limit_bytes=59000000),
        cost_estimate=pl.CostEstimate(flops=FIRST * 4 * CAP * HID * FF, bytes_accessed=48 * 1024 * 1024, transcendentals=0),
        name='weight_grads_a',
    )(xl, da, u, dh, y, gg, loss)


def gradx_kernel(scale, late_in, now_v, r_v, tab_in, gw_v, gx, late_v, tab_v, gx_v, in_sem, out_sem):
    def pieces(c):
        cols = pl.ds(c * CH, CH)
        out = [pltpu.make_async_copy(late_in.at[:, :, cols], late_v.at[:, :, cols], in_sem.at[c])]
        if c >= NOW:
            more = pl.ds((NCH + c - NOW) * CH, CH)
            out.append(pltpu.make_async_copy(late_in.at[:, :, more], late_v.at[:, :, more], in_sem.at[c]))
        return out
    cp_tab = pltpu.make_async_copy(tab_in, tab_v, in_sem.at[NCH])
    cp_tab.start()
    for c in range(NCH):
        for cp in pieces(c):
            cp.start()
    cp_tab.wait()
    for c in range(NCH):
        cols = pl.ds(c * CH, CH)
        tot = r_v[:, cols].astype(F32) * scale + dot(tab_v[:, 512:576], gw_v[:, cols])
        if c < NOW:
            tot = tot + dot(tab_v[:, 256:512], now_v[:, :, cols].reshape(256, CH))
        for cp in pieces(c):
            cp.wait()
        if c >= NOW:
            tot = tot + dot(tab_v[:, 256:512], late_v[:, :, pl.ds((NCH + c - NOW) * CH, CH)].reshape(256, CH))
        gx_v[:, cols] = (tot + dot(tab_v[:, 0:256], late_v[:, :, cols].reshape(256, CH))).astype(BF)
        pltpu.make_async_copy(gx_v.at[:, cols], gx.at[:, cols], out_sem).start()
    for c in range(NCH):
        cols = pl.ds(c * CH, CH)
        pltpu.make_async_copy(gx_v.at[:, cols], gx.at[:, cols], out_sem).wait()


def gradx_call(late, now, r, tab, gw, scale):
    any_ = pl.BlockSpec(memory_space=pl.ANY)
    vmem = pl.BlockSpec(memory_space=pltpu.VMEM)
    hbm = pl.BlockSpec(memory_space=pltpu.HBM)
    V = pltpu.VMEM
    return pl.pallas_call(
        functools.partial(gradx_kernel, scale),
        in_specs=[hbm, vmem, vmem, hbm, vmem],
        out_specs=any_,
        out_shape=jax.ShapeDtypeStruct((TOK, HID), BF),
        scratch_shapes=[V((N, 16, 2 * HID - NOW * CH), BF), V((TOK, 640), BF), V((TOK, HID), BF), pltpu.SemaphoreType.DMA((NCH + 1,)),
                        pltpu.SemaphoreType.DMA],
        compiler_params=pltpu.CompilerParams(vmem_limit_bytes=16000000),
        name='grad_x',
    )(late, now, r, tab, gw)


def solution(mesh):
    def device_step(x, gate_w, up_w, down_w, expert_picks, loss_w):
        scale = 1.0 / math.sqrt(TOK * N * HID)
        gate_t = gate_w.T
        y, now, later, tab, gg, loss, xl, u, dh, da = comm_call(expert_picks, x, gate_t, up_w, down_w, loss_w, scale)
        later = lax.all_to_all(later, 'ep', 0, 0, tiled=True)
        grad_up, grad_down, y, gg, loss = wgrad1_call(xl, da, u, dh, y, gg, loss)
        grad_x = gradx_call(later, now, loss_w, tab, gate_t, scale)
        return y.reshape(TOK, HID), loss[0, 0], grad_x, grad_up, grad_down, gg.T

    return jax.shard_map(device_step, mesh=mesh,
                         in_specs=(P('ep'), P(), P('ep'), P('ep'), P('ep'), P('ep')),
                         out_specs=(P('ep'), P(), P('ep'), P('ep'), P('ep'), P()),
                         check_vma=False)
```

profile of v0, /device:TPU:0, one launch (start us, length us, event | category | flops | bytes accessed | tf_op | source)
XLA Modules:
  0.0 102.6 jit_solution(2589501918584408781)
XLA Ops:
  0.6 74.0 %exchange.1 = (bf16[16,16,2048]{2,1,0:T(8,128)(2,1)}, bf16[16,16,1024]{2,1,0:T(8,128)(2,1)}, bf16[16,16,3072]{2,1,0:T(8,128)(2,1)}, bf16[256,640]{1,0:T(8,128)(2...) custom-call(s32[4,128]{1,0:T(4,128)} %sel_ref.1, ...), custom_call_target="tpu_custom_call" | custom-call | tf_op jit(solution)/shard_map/exchange/pallas_call | solution.py:431
  74.6 2.5 %all-to-all-start = ((bf16[16,16,3072]{2,1,0:T(8,128)(2,1)}), bf16[16,16,3072]{2,1,0:T(8,128)(2,1)S(1)}, u32[]{:S(2)}, u32[]{:S(2)}) async-start(bf16[16,16,3072]{2,1,0:T(8,128)(2,1)} %get-tuple-element.30), calls=%async_computation | async-start | bytes 3145728 | tf_op jit(solution)/shard_map/all_to_all | solution.py:590
  77.1 0.0 copy-start
  77.1 0.0 copy-start.1
  77.1 0.0 copy-start.2
  77.1 19.6 %weight_grads_a.1 = (bf16[4,2048,1408]{2,1,0:T(8,128)(2,1)}, bf16[4,1408,2048]{2,1,0:T(8,128)(2,1)}, bf16[16,16,2048]{2,1,0:T(8,128)(2,1)}, f32[64,2048]{1,0:T(8,128)}, f32[1,1]{1,0:T(1,128)}) custom-call(bf16[4,128,2048]{2,1,0:T(8,128)(2,1)} %get-tuple-element.21.xl_in, bf16[4,128,1408]{2,1,0:T(8,128)(2,1)} %get-tuple-element.22.da_in, ...), custom_call_target="tpu_custom_call" | custom-call | flops 5905580032 | bytes 50331648 | tf_op jit(solution)/shard_map/weight_grads_a/pallas_call | solution.py:524
  96.8 2.5 %all-to-all-done.late_in = bf16[16,16,3072]{2,1,0:T(8,128)(2,1)S(1)} async-done(((bf16[16,16,3072]{2,1,0:T(8,128)(2,1)}), bf16[16,16,3072]{2,1,0:T(8,128)(2,1)S(1)}, u32[]{:S(2)}, u32[]{:S(2)}) %all-to-all-start) | async-done | bytes 1572896 | tf_op jit(solution)/shard_map/all_to_all | solution.py:590
  99.2 0.0 copy-done
  99.3 0.0 copy-done.1
  99.3 0.0 copy-done.2
  99.3 0.0 copy-start.3
  99.3 1.0 copy-done.3
  100.2 2.4 %grad_x.1 = bf16[256,2048]{1,0:T(8,128)(2,1)} custom-call(bf16[16,16,3072]{2,1,0:T(8,128)(2,1)S(1)} %all-to-all-done.late_in, bf16[16,16,1024]{2,1,0:T(8,128)(2,1)S(1)} %copy-done.2, bf16[256,2048]{1,0:T(8,128)(2,1)S(1)} %copy-done, bf16[256,640]{1,0:T(8,128)(2,1)S(1)} %copy-done.3, bf16[64,2048]{1,0:T(8,128)(2,1)S(1)} %bitcast.5), custom_call_target="tpu_custom_call" | custom-call | tf_op jit(solution)/shard_map/grad_x/pallas_call | solution.py:573
Async XLA Ops:
  74.6 24.6 %all-to-all-start = ((bf16[16,16,3072]{2,1,0:T(8,128)(2,1)}), bf16[16,16,3072]{2,1,0:T(8,128)(2,1)S(1)}, u32[]{:S(2)}, u32[]{:S(2)}) async-start(bf16[16,16,3072]{2,1,0:T(8,128)(2,1)} %get-tuple-element.30), calls=%async_computation | async-start | bytes 3145728 | tf_op jit(solution)/shard_map/all_to_all | solution.py:590
  77.1 22.1 %copy-start = (bf16[256,2048]{1,0:T(8,128)(2,1)S(1)}, bf16[256,2048]{1,0:T(8,128)(2,1)}, u32[]{:S(2)}) copy-start(bf16[256,2048]{1,0:T(8,128)(2,1)} %r_v.1) | copy-start | bytes 3145732
  77.1 22.1 %copy-start.1 = (bf16[2048,64]{0,1:T(8,128)(2,1)S(1)}, bf16[2048,64]{0,1:T(8,128)(2,1)}, u32[]{:S(2)}) copy-start(bf16[2048,64]{0,1:T(8,128)(2,1)} %param.7) | copy-start | bytes 786436
  77.1 22.1 %copy-start.2 = (bf16[16,16,1024]{2,1,0:T(8,128)(2,1)S(1)}, bf16[16,16,1024]{2,1,0:T(8,128)(2,1)}, u32[]{:S(2)}) copy-start(bf16[16,16,1024]{2,1,0:T(8,128)(2,1)} %get-tuple-element.31.now_v) | copy-start | bytes 1572868
  99.3 1.0 copy-start.3
where the time goes:
time: 103 us
  Pallas kernels  96 us (93%)
  waiting for transfers between devices  2.47 us (2%)
  starting transfers between devices  2.46 us (2%)
    pallas_call x1, Pallas kernels, comm_call(): pl.pallas_call(functools.partial(comm_kernel, scale), out_shape=[shape((N...  74 us
    pallas_call x1, Pallas kernels, wgrad1_call(): pl.pallas_call(wgrad1_kernel, in_specs=[any_] * 6 + [smem], out_specs=[an...  19.6 us
    all_to_all x1, waiting for transfers between devices, device_step(): later = lax.all_to_all(later, 'ep', 0, 0, tiled=True)  2.47 us
    all_to_all x1, starting transfers between devices, device_step(): later = lax.all_to_all(later, 'ep', 0, 0, tiled=True)  2.46 us
    pallas_call x1, Pallas kernels, gradx_call(): pl.pallas_call(functools.partial(gradx_kernel, scale), in_specs=[hbm, vme...  2.39 us
  transfers between devices with their start and end apart: 1, of which 1 were waited for; matrix products, arithmetic and copies ran while one was open for 0% of the time, Pallas kernels for 19%

commit v1 on v0

--- a/solution.py
+++ b/solution.py
@@ -21,7 +21,7 @@
 FIRST = 4
 HALF = HID // 2
 NOW = 2
-ORDER = (14, 15, 6, 10, 12, 7, 11, 13, 2, 4, 8, 3, 5, 9, 1)
+ORDER = (14, 12, 8, 15, 13, 9, 6, 4, 7, 5, 10, 11, 2, 3, 1)
 
 
 def dot(a, b, ca=1, cb=0):

time: 103 us -> 103 us (level)
  no operation moved by 1% of the time
where the time goes in v1:
time: 103 us; the launch traced here: 102 us
  Pallas kernels  95.8 us (93%)
  starting transfers between devices  2.48 us (2%)
  waiting for transfers between devices  2.32 us (2%)
    pallas_call x1, Pallas kernels, comm_call(): pl.pallas_call(functools.partial(comm_kernel, scale), out_shape=[shape((N...  73.8 us
    pallas_call x1, Pallas kernels, wgrad1_call(): pl.pallas_call(wgrad1_kernel, in_specs=[any_] * 6 + [smem], out_specs=[an...  19.6 us
    all_to_all x1, starting transfers between devices, device_step(): later = lax.all_to_all(later, 'ep', 0, 0, tiled=True)  2.48 us
    pallas_call x1, Pallas kernels, gradx_call(): pl.pallas_call(functools.partial(gradx_kernel, scale), in_specs=[hbm, vme...  2.38 us
    all_to_all x1, waiting for transfers between devices, device_step(): later = lax.all_to_all(later, 'ep', 0, 0, tiled=True)  2.32 us
  transfers between devices with their start and end apart: 1, of which 1 were waited for; matrix products, arithmetic and copies ran while one was open for 0% of the time, Pallas kernels for 19%

profile of v1, /device:TPU:0, one launch (start us, length us, event | category | flops | bytes accessed | tf_op | source)
XLA Modules:
  0.0 102.3 jit_solution(276033669419146530)
XLA Ops:
  0.6 73.8 %exchange.1 = (bf16[16,16,2048]{2,1,0:T(8,128)(2,1)}, bf16[16,16,1024]{2,1,0:T(8,128)(2,1)}, bf16[16,16,3072]{2,1,0:T(8,128)(2,1)}, bf16[256,640]{1,0:T(8,128)(2...) custom-call(s32[4,128]{1,0:T(4,128)} %sel_ref.1, ...), custom_call_target="tpu_custom_call" | custom-call | tf_op jit(solution)/shard_map/exchange/pallas_call | solution.py:431
  74.4 2.5 %all-to-all-start = ((bf16[16,16,3072]{2,1,0:T(8,128)(2,1)}), bf16[16,16,3072]{2,1,0:T(8,128)(2,1)S(1)}, u32[]{:S(2)}, u32[]{:S(2)}) async-start(bf16[16,16,3072]{2,1,0:T(8,128)(2,1)} %get-tuple-element.30), calls=%async_computation | async-start | bytes 3145728 | tf_op jit(solution)/shard_map/all_to_all | solution.py:590
  76.9 0.0 copy-start
  76.9 0.0 copy-start.1
  76.9 0.0 copy-start.2
  77.0 19.6 %weight_grads_a.1 = (bf16[4,2048,1408]{2,1,0:T(8,128)(2,1)}, bf16[4,1408,2048]{2,1,0:T(8,128)(2,1)}, bf16[16,16,2048]{2,1,0:T(8,128)(2,1)}, f32[64,2048]{1,0:T(8,128)}, f32[1,1]{1,0:T(1,128)}) custom-call(bf16[4,128,2048]{2,1,0:T(8,128)(2,1)} %get-tuple-element.21.xl_in, bf16[4,128,1408]{2,1,0:T(8,128)(2,1)} %get-tuple-element.22.da_in, ...), custom_call_target="tpu_custom_call" | custom-call | flops 5905580032 | bytes 50331648 | tf_op jit(solution)/shard_map/weight_grads_a/pallas_call | solution.py:524
  96.6 2.3 %all-to-all-done.late_in = bf16[16,16,3072]{2,1,0:T(8,128)(2,1)S(1)} async-done(((bf16[16,16,3072]{2,1,0:T(8,128)(2,1)}), bf16[16,16,3072]{2,1,0:T(8,128)(2,1)S(1)}, u32[]{:S(2)}, u32[]{:S(2)}) %all-to-all-start) | async-done | bytes 1572896 | tf_op jit(solution)/shard_map/all_to_all | solution.py:590
  98.9 0.0 copy-done
  98.9 0.0 copy-done.1
  98.9 0.0 copy-done.2
  98.9 0.0 copy-start.3
  98.9 1.0 copy-done.3
  99.9 2.4 %grad_x.1 = bf16[256,2048]{1,0:T(8,128)(2,1)} custom-call(bf16[16,16,3072]{2,1,0:T(8,128)(2,1)S(1)} %all-to-all-done.late_in, bf16[16,16,1024]{2,1,0:T(8,128)(2,1)S(1)} %copy-done.2, bf16[256,2048]{1,0:T(8,128)(2,1)S(1)} %copy-done, bf16[256,640]{1,0:T(8,128)(2,1)S(1)} %copy-done.3, bf16[64,2048]{1,0:T(8,128)(2,1)S(1)} %bitcast.5), custom_call_target="tpu_custom_call" | custom-call | tf_op jit(solution)/shard_map/grad_x/pallas_call | solution.py:573
Async XLA Ops:
  74.4 24.5 %all-to-all-start = ((bf16[16,16,3072]{2,1,0:T(8,128)(2,1)}), bf16[16,16,3072]{2,1,0:T(8,128)(2,1)S(1)}, u32[]{:S(2)}, u32[]{:S(2)}) async-start(bf16[16,16,3072]{2,1,0:T(8,128)(2,1)} %get-tuple-element.30), calls=%async_computation | async-start | bytes 3145728 | tf_op jit(solution)/shard_map/all_to_all | solution.py:590
  76.9 22.0 %copy-start = (bf16[256,2048]{1,0:T(8,128)(2,1)S(1)}, bf16[256,2048]{1,0:T(8,128)(2,1)}, u32[]{:S(2)}) copy-start(bf16[256,2048]{1,0:T(8,128)(2,1)} %r_v.1) | copy-start | bytes 3145732
  76.9 22.0 %copy-start.1 = (bf16[2048,64]{0,1:T(8,128)(2,1)S(1)}, bf16[2048,64]{0,1:T(8,128)(2,1)}, u32[]{:S(2)}) copy-start(bf16[2048,64]{0,1:T(8,128)(2,1)} %param.7) | copy-start | bytes 786436
  76.9 22.0 %copy-start.2 = (bf16[16,16,1024]{2,1,0:T(8,128)(2,1)S(1)}, bf16[16,16,1024]{2,1,0:T(8,128)(2,1)}, u32[]{:S(2)}) copy-start(bf16[16,16,1024]{2,1,0:T(8,128)(2,1)} %get-tuple-element.31.now_v) | copy-start | bytes 1572868
  98.9 1.0 copy-start.3

commit v2 on v1

--- a/solution.py
+++ b/solution.py
@@ -55,10 +55,10 @@
 
 
 def comm_kernel(scale, sel_ref, x_hbm, gw_hbm, up_hbm, dn_hbm, r_hbm,
-                y_out, gnow_out, glater_out, tab_out, gg_out, loss_out, xl_out, u_out, dh_out, da_out,
+                y_out, tab_out, glater_out, gg_out, loss_out, xl_out, u_out, dh_out, da_out,
                 x_v, r_v, gw_v, w1, w2, xsend, rsend, xrecv, rrecv, hsend, hrecv, gsend,
                 xl_v, dh_v, u_v, gp_v, da_v, ggpart, ggpair, gghalf, ggrecv, ggall, selsend, selall, gates, gates_all,
-                losssend, lossall, dgsend, dgall, one_v, c_v, e_v, probs_v, dlog_v,
+                losssend, lossall, dgsend, dgall, one_v, c_v, e_v, probs_v, dlog_v, ids_v,
                 ld_sem, w_sem, out_sem, send_sem, recv_sem):
     me = lax.axis_index('ep')
     peers = [flip(me, k) for k in ORDER]
@@ -163,6 +163,9 @@
         for p in peers:
             push(xsend.at[p, :, cols], xrecv.at[me, :, cols], p, 1).start()
     xrecv[pl.ds(me, 1)] = xsend[pl.ds(me, 1)]
+
+    rows16 = jnp.where(iota((16, 512), 1) // 64 == iota((16, 512), 0), jnp.broadcast_to(ids, (16, 512)), 0.0).astype(BF)
+    ids_v[...] = dot(rows16, ones_where(iota((512, 128), 1) == 64 + iota((512, 128), 0) % 64))
 
     rep = ones_where(iota((64, 512), 0) == 4 * ((iota((64, 512), 1) % 256) // 16) + 2 * (iota((64, 512), 1) // 256)
                      + (iota((64, 512), 1) % 16) // 8)
@@ -238,9 +241,10 @@
 
     def send_now(c):
         cols = pl.ds(c * CH, CH)
+        mine_rows = pl.ds(pl.multiple_of(me * 16, 16), 16)
         for p in peers:
-            push(gsend.at[1, p, :, cols], gnow_out.at[me, :, cols], p, 5).start()
-        pltpu.make_async_copy(gsend.at[1, me, :, cols], gnow_out.at[me, :, cols], out_sem.at[0]).start()
+            push(gsend.at[1, p, :, cols], tab_out.at[mine_rows, cols], p, 5).start()
+        pltpu.make_async_copy(gsend.at[1, me, :, cols], tab_out.at[mine_rows, cols], out_sem.at[0]).start()
 
     lane128 = iota((CAP, 128), 1)
     rows = jnp.broadcast_to(gates_all[...], (N, 8, 512)).reshape(CAP, 512)
@@ -286,7 +290,9 @@
             ds = ds + dot(one_v[...], term)
         probs = probs_v[...]
         dlog = (probs * (ds - jnp.sum(probs * ds, axis=1, keepdims=True))).astype(BF)
-        dlog_v[...] = jnp.concatenate([dlog, jnp.zeros_like(dlog)], axis=1)
+        wide_d = jnp.concatenate([dlog, jnp.zeros_like(dlog)], axis=1)
+        dlog_v[...] = wide_d
+        dlog_v[0:16, :] = (wide_d[0:16].astype(F32) + ids_v[...]).astype(BF)
         dlog_t = dlog.astype(F32).T.astype(BF)
         for c in range(NCH):
             part = dot(dlog_t, x_v[:, c * CH:(c + 1) * CH])
@@ -360,10 +366,8 @@
     pltpu.make_async_copy(dh_v, dh_out, out_sem.at[0]).start()
     pltpu.make_async_copy(da_v, da_out, out_sem.at[0]).start()
 
-    cp_dlog = pltpu.make_async_copy(dlog_v, tab_out.at[:, pl.ds(512, 128)], out_sem.at[0])
+    cp_dlog = pltpu.make_async_copy(dlog_v, tab_out.at[:, pl.ds(NOW * CH, 128)], out_sem.at[0])
     cp_dlog.start()
-    cp_one = pltpu.make_async_copy(one_v, tab_out.at[:, pl.ds(0, 512)], out_sem.at[0])
-    cp_one.start()
 
     gate_gather()
 
@@ -393,7 +397,8 @@
         cp.start()
     wait_recv(lossall, 7)
     loss_out[0, 0] = jnp.sum(lossall[...]) * scale
-    wait_recv(gnow_out, 5)
+    part = tab_out.at[pl.ds(0, (N - 1) * 16), pl.ds(0, NOW * CH)]
+    pltpu.make_async_copy(part, part, recv_sem.at[5]).wait()
 
     wait_send(selall, 0)
     wait_send(gates_all, 2)
@@ -403,7 +408,7 @@
     pltpu.make_async_copy(part, part, send_sem.at[1]).wait()
     for c in range(NOW):
         cols = pl.ds(c * CH, CH)
-        pltpu.make_async_copy(gsend.at[1, me, :, cols], gnow_out.at[me, :, cols], out_sem.at[0]).wait()
+        pltpu.make_async_copy(gsend.at[1, me, :, cols], tab_out.at[pl.ds(pl.multiple_of(me * 16, 16), 16), cols], out_sem.at[0]).wait()
     wait_send(rsend, 3)
     wait_send(lossall, 7)
     push(ggpart.at[1 - core], ggpair, twin, 8).wait_send()
@@ -413,7 +418,6 @@
     for cp in later:
         cp.wait()
     cp_dlog.wait()
-    cp_one.wait()
     pltpu.make_async_copy(xl_v, xl_out, out_sem.at[0]).wait()
     pltpu.make_async_copy(u_v, u_out, out_sem.at[0]).wait()
     pltpu.make_async_copy(dh_v, dh_out, out_sem.at[0]).wait()
@@ -430,11 +434,11 @@
     shape = jax.ShapeDtypeStruct
     return pl.pallas_call(
         functools.partial(comm_kernel, scale),
-        out_shape=[shape((N, 16, HID), BF), shape((N, 16, NOW * CH), BF), shape((N, 16, 2 * HID - NOW * CH), BF), shape((TOK, 640), BF),
+        out_shape=[shape((N, 16, HID), BF), shape((TOK, NOW * CH + 128), BF), shape((N, 16, 2 * HID - NOW * CH), BF),
                    shape((64, HID), F32), shape((1, 1), F32),
                    shape((LE, CAP, HID), BF), shape((LE, CAP, FF), BF), shape((LE, CAP, HID), BF), shape((LE, CAP, FF), BF)],
         in_specs=[vmem, any_, any_, any_, any_, any_],
-        out_specs=[any_, any_, any_, any_, any_, pl.BlockSpec(memory_space=pltpu.SMEM), any_, any_, any_, any_],
+        out_specs=[any_, any_, any_, any_, pl.BlockSpec(memory_space=pltpu.SMEM), any_, any_, any_, any_],
         scratch_shapes=[
             V((TOK, HID), BF), V((TOK, HID), BF), V((64, HID), BF),
             V((3, HID, FF), BF), V((3, FF, HID), BF),
@@ -444,7 +448,7 @@
             V((2, 8, 64, 128), F32), V((8, 64, 128), F32), V((8, 64, 128), F32), V((8, 64, 128), F32), V((2, 8, 64, 128), F32),
             V((8, CAP), jnp.int32), V((N, 8, CAP), jnp.int32), V((1, 512), F32), V((N, 1, 512), F32),
             V((1, CH), F32), V((N, 1, CH), F32), V((N, 8, 128), F32), V((N, 8, 128), F32),
-            V((TOK, 512), BF), V((3, TOK, 512), BF), V((LE, CAP, TOK), BF), V((TOK, 64), F32), V((TOK, 128), BF),
+            V((TOK, 512), BF), V((3, TOK, 512), BF), V((LE, CAP, TOK), BF), V((TOK, 64), F32), V((TOK, 128), BF), V((16, 128), F32),
             pltpu.SemaphoreType.DMA((2,)), pltpu.SemaphoreType.DMA((2, 3)), pltpu.SemaphoreType.DMA((1,)),
             pltpu.SemaphoreType.DMA((2,)), pltpu.SemaphoreType.DMA((12,)),
         ],
@@ -535,7 +539,7 @@
     )(xl, da, u, dh, y, gg, loss)
 
 
-def gradx_kernel(scale, late_in, now_v, r_v, tab_in, gw_v, gx, late_v, tab_v, gx_v, in_sem, out_sem):
+def gradx_kernel(scale, late_in, r_v, tab_v, gw_v, gx, late_v, gx_v, in_sem, out_sem):
     def pieces(c):
         cols = pl.ds(c * CH, CH)
         out = [pltpu.make_async_copy(late_in.at[:, :, cols], late_v.at[:, :, cols], in_sem.at[c])]
@@ -543,53 +547,53 @@
             more = pl.ds((NCH + c - NOW) * CH, CH)
             out.append(pltpu.make_async_copy(late_in.at[:, :, more], late_v.at[:, :, more], in_sem.at[c]))
         return out
-    cp_tab = pltpu.make_async_copy(tab_in, tab_v, in_sem.at[NCH])
-    cp_tab.start()
     for c in range(NCH):
         for cp in pieces(c):
             cp.start()
-    cp_tab.wait()
+    block = tab_v[0:16, NOW * CH:NOW * CH + 128]
+    rows16 = dot(block, ones_where(iota((128, 512), 0) == 64 + iota((128, 512), 1) % 64))
+    ids = jnp.sum(jnp.where(iota((16, 512), 1) // 64 == iota((16, 512), 0), rows16, 0.0), axis=0, keepdims=True)
+    one = jnp.where(iota((TOK, 512), 0).astype(F32) == ids, 1.0, 0.0).astype(BF)
+    dlog = tab_v[:, NOW * CH:NOW * CH + 64]
     for c in range(NCH):
         cols = pl.ds(c * CH, CH)
-        tot = r_v[:, cols].astype(F32) * scale + dot(tab_v[:, 512:576], gw_v[:, cols])
+        tot = r_v[:, cols].astype(F32) * scale + dot(dlog, gw_v[:, cols])
         if c < NOW:
-            tot = tot + dot(tab_v[:, 256:512], now_v[:, :, cols].reshape(256, CH))
+            tot = tot + dot(one[:, 256:512], tab_v[:, cols])
         for cp in pieces(c):
             cp.wait()
         if c >= NOW:
-            tot = tot + dot(tab_v[:, 256:512], late_v[:, :, pl.ds((NCH + c - NOW) * CH, CH)].reshape(256, CH))
-        gx_v[:, cols] = (tot + dot(tab_v[:, 0:256], late_v[:, :, cols].reshape(256, CH))).astype(BF)
+            tot = tot + dot(one[:, 256:512], late_v[:, :, pl.ds((NCH + c - NOW) * CH, CH)].reshape(256, CH))
+        gx_v[:, cols] = (tot + dot(one[:, 0:256], late_v[:, :, cols].reshape(256, CH))).astype(BF)
         pltpu.make_async_copy(gx_v.at[:, cols], gx.at[:, cols], out_sem).start()
     for c in range(NCH):
         cols = pl.ds(c * CH, CH)
         pltpu.make_async_copy(gx_v.at[:, cols], gx.at[:, cols], out_sem).wait()
 
 
-def gradx_call(late, now, r, tab, gw, scale):
+def gradx_call(late, r, tab, gw, scale):
     any_ = pl.BlockSpec(memory_space=pl.ANY)
     vmem = pl.BlockSpec(memory_space=pltpu.VMEM)
-    hbm = pl.BlockSpec(memory_space=pltpu.HBM)
     V = pltpu.VMEM
     return pl.pallas_call(
         functools.partial(gradx_kernel, scale),
-        in_specs=[hbm, vmem, vmem, hbm, vmem],
+        in_specs=[any_, vmem, vmem, vmem],
         out_specs=any_,
         out_shape=jax.ShapeDtypeStruct((TOK, HID), BF),
-        scratch_shapes=[V((N, 16, 2 * HID - NOW * CH), BF), V((TOK, 640), BF), V((TOK, HID), BF), pltpu.SemaphoreType.DMA((NCH + 1,)),
-                        pltpu.SemaphoreType.DMA],
+        scratch_shapes=[V((N, 16, 2 * HID - NOW * CH), BF), V((TOK, HID), BF), pltpu.SemaphoreType.DMA((NCH,)), pltpu.SemaphoreType.DMA],
         compiler_params=pltpu.CompilerParams(vmem_limit_bytes=16000000),
         name='grad_x',
-    )(late, now, r, tab, gw)
+    )(late, r, tab, gw)
 
 
 def solution(mesh):
     def device_step(x, gate_w, up_w, down_w, expert_picks, loss_w):
         scale = 1.0 / math.sqrt(TOK * N * HID)
         gate_t = gate_w.T
-        y, now, later, tab, gg, loss, xl, u, dh, da = comm_call(expert_picks, x, gate_t, up_w, down_w, loss_w, scale)
+        y, tab, later, gg, loss, xl, u, dh, da = comm_call(expert_picks, x, gate_t, up_w, down_w, loss_w, scale)
         later = lax.all_to_all(later, 'ep', 0, 0, tiled=True)
         grad_up, grad_down, y, gg, loss = wgrad1_call(xl, da, u, dh, y, gg, loss)
-        grad_x = gradx_call(later, now, loss_w, tab, gate_t, scale)
+        grad_x = gradx_call(later, loss_w, tab, gate_t, scale)
         return y.reshape(TOK, HID), loss[0, 0], grad_x, grad_up, grad_down, gg.T
 
     return jax.shard_map(device_step, mesh=mesh,

time: 103 us -> 104 us (level)
  Pallas kernels: 95.8 us -> 98.7 us
    pallas_call x1, Pallas kernels: 73.8 us -> 76.7 us  [comm_call(): pl.pallas_call(functools.partial(comm_kernel, scale), out_shape=[shape((N...]
where the time goes in v2:
time: 104 us
  Pallas kernels  98.7 us (95%)
  starting transfers between devices  2.46 us (2%)
  waiting for transfers between devices  2.35 us (2%)
    pallas_call x1, Pallas kernels, comm_call(): pl.pallas_call(functools.partial(comm_kernel, scale), out_shape=[shape((N...  76.7 us
    pallas_call x1, Pallas kernels, wgrad1_call(): pl.pallas_call(wgrad1_kernel, in_specs=[any_] * 6 + [smem], out_specs=[an...  19.8 us
    all_to_all x1, starting transfers between devices, device_step(): later = lax.all_to_all(later, 'ep', 0, 0, tiled=True)  2.46 us
    all_to_all x1, waiting for transfers between devices, device_step(): later = lax.all_to_all(later, 'ep', 0, 0, tiled=True)  2.35 us
    pallas_call x1, Pallas kernels, gradx_call(): pl.pallas_call(functools.partial(gradx_kernel, scale), in_specs=[any_, vm...  2.29 us
  transfers between devices with their start and end apart: 1, of which 1 were waited for; matrix products, arithmetic and copies ran while one was open for 0% of the time, Pallas kernels for 19%

profile of v2, /device:TPU:0, one launch (start us, length us, event | category | flops | bytes accessed | tf_op | source)
XLA Modules:
  0.0 104.2 jit_solution(10708209029779422581)
XLA Ops:
  0.6 76.7 %exchange.1 = (bf16[16,16,2048]{2,1,0:T(8,128)(2,1)}, bf16[256,1152]{1,0:T(8,128)(2,1)}, bf16[16,16,3072]{2,1,0:T(8,128)(2,1)}, f32[64,2048]{1,0:T(8,128)}, f32[...) custom-call(s32[4,128]{1,0:T(4,128)} %sel_ref.1, ...), custom_call_target="tpu_custom_call" | custom-call | tf_op jit(solution)/shard_map/exchange/pallas_call | solution.py:435
  77.3 2.5 %all-to-all-start = ((bf16[16,16,3072]{2,1,0:T(8,128)(2,1)}), bf16[16,16,3072]{2,1,0:T(8,128)(2,1)S(1)}, u32[]{:S(2)}, u32[]{:S(2)}) async-start(bf16[16,16,3072]{2,1,0:T(8,128)(2,1)} %get-tuple-element.29), calls=%async_computation | async-start | bytes 3145728 | tf_op jit(solution)/shard_map/all_to_all | solution.py:594
  79.8 0.0 copy-start
  79.8 0.0 copy-start.1
  79.8 0.0 copy-start.2
  79.8 19.8 %weight_grads_a.1 = (bf16[4,2048,1408]{2,1,0:T(8,128)(2,1)}, bf16[4,1408,2048]{2,1,0:T(8,128)(2,1)}, bf16[16,16,2048]{2,1,0:T(8,128)(2,1)}, f32[64,2048]{1,0:T(8,128)}, f32[1,1]{1,0:T(1,128)}) custom-call(bf16[4,128,2048]{2,1,0:T(8,128)(2,1)} %get-tuple-element.20.xl_in, bf16[4,128,1408]{2,1,0:T(8,128)(2,1)} %get-tuple-element.21.da_in, ...), custom_call_target="tpu_custom_call" | custom-call | flops 5905580032 | bytes 50331648 | tf_op jit(solution)/shard_map/weight_grads_a/pallas_call | solution.py:528
  99.6 2.4 %all-to-all-done.late_in = bf16[16,16,3072]{2,1,0:T(8,128)(2,1)S(1)} async-done(((bf16[16,16,3072]{2,1,0:T(8,128)(2,1)}), bf16[16,16,3072]{2,1,0:T(8,128)(2,1)S(1)}, u32[]{:S(2)}, u32[]{:S(2)}) %all-to-all-start) | async-done | bytes 1572896 | tf_op jit(solution)/shard_map/all_to_all | solution.py:594
  101.9 0.0 copy-done
  101.9 0.0 copy-done.1
  101.9 0.0 copy-done.2
  101.9 2.3 %grad_x.1 = bf16[256,2048]{1,0:T(8,128)(2,1)} custom-call(bf16[16,16,3072]{2,1,0:T(8,128)(2,1)S(1)} %all-to-all-done.late_in, bf16[256,2048]{1,0:T(8,128)(2,1)S(1)} %copy-done, bf16[256,1152]{1,0:T(8,128)(2,1)S(1)} %copy-done.2, bf16[64,2048]{1,0:T(8,128)(2,1)S(1)} %bitcast.5), custom_call_target="tpu_custom_call" | custom-call | tf_op jit(solution)/shard_map/grad_x/pallas_call | solution.py:578
Async XLA Ops:
  77.3 24.6 %all-to-all-start = ((bf16[16,16,3072]{2,1,0:T(8,128)(2,1)}), bf16[16,16,3072]{2,1,0:T(8,128)(2,1)S(1)}, u32[]{:S(2)}, u32[]{:S(2)}) async-start(bf16[16,16,3072]{2,1,0:T(8,128)(2,1)} %get-tuple-element.29), calls=%async_computation | async-start | bytes 3145728 | tf_op jit(solution)/shard_map/all_to_all | solution.py:594
  79.8 22.1 %copy-start = (bf16[256,2048]{1,0:T(8,128)(2,1)S(1)}, bf16[256,2048]{1,0:T(8,128)(2,1)}, u32[]{:S(2)}) copy-start(bf16[256,2048]{1,0:T(8,128)(2,1)} %r_v.1) | copy-start | bytes 3145732
  79.8 22.1 %copy-start.1 = (bf16[2048,64]{0,1:T(8,128)(2,1)S(1)}, bf16[2048,64]{0,1:T(8,128)(2,1)}, u32[]{:S(2)}) copy-start(bf16[2048,64]{0,1:T(8,128)(2,1)} %param.7) | copy-start | bytes 786436
  79.8 22.1 %copy-start.2 = (bf16[256,1152]{1,0:T(8,128)(2,1)S(1)}, bf16[256,1152]{1,0:T(8,128)(2,1)}, u32[]{:S(2)}) copy-start(bf16[256,1152]{1,0:T(8,128)(2,1)} %get-tuple-element.30.tab_v) | copy-start | bytes 1769476

commit v3 on v2

--- a/solution.py
+++ b/solution.py
@@ -55,7 +55,7 @@
 
 
 def comm_kernel(scale, sel_ref, x_hbm, gw_hbm, up_hbm, dn_hbm, r_hbm,
-                y_out, tab_out, glater_out, gg_out, loss_out, xl_out, u_out, dh_out, da_out,
+                y_out, gnow_out, glater_out, tab_out, gg_out, loss_out, xl_out, u_out, dh_out, da_out,
                 x_v, r_v, gw_v, w1, w2, xsend, rsend, xrecv, rrecv, hsend, hrecv, gsend,
                 xl_v, dh_v, u_v, gp_v, da_v, ggpart, ggpair, gghalf, ggrecv, ggall, selsend, selall, gates, gates_all,
                 losssend, lossall, dgsend, dgall, one_v, c_v, e_v, probs_v, dlog_v, ids_v,
@@ -164,9 +164,6 @@
             push(xsend.at[p, :, cols], xrecv.at[me, :, cols], p, 1).start()
     xrecv[pl.ds(me, 1)] = xsend[pl.ds(me, 1)]
 
-    rows16 = jnp.where(iota((16, 512), 1) // 64 == iota((16, 512), 0), jnp.broadcast_to(ids, (16, 512)), 0.0).astype(BF)
-    ids_v[...] = dot(rows16, ones_where(iota((512, 128), 1) == 64 + iota((512, 128), 0) % 64))
-
     rep = ones_where(iota((64, 512), 0) == 4 * ((iota((64, 512), 1) % 256) // 16) + 2 * (iota((64, 512), 1) // 256)
                      + (iota((64, 512), 1) % 16) // 8)
     wide = 0.0
@@ -185,6 +182,9 @@
     for p in peers:
         push(rsend.at[p], rrecv.at[me], p, 3).start()
     rrecv[pl.ds(me, 1)] = rsend[pl.ds(me, 1)]
+
+    rows16 = jnp.where(iota((16, 512), 1) // 64 == iota((16, 512), 0), jnp.broadcast_to(ids, (16, 512)), 0.0).astype(BF)
+    ids_v[...] = dot(rows16, ones_where(iota((512, 128), 1) == 64 + iota((512, 128), 0) % 64))
 
     wait_recv(xrecv, 1)
 
@@ -241,10 +241,9 @@
 
     def send_now(c):
         cols = pl.ds(c * CH, CH)
-        mine_rows = pl.ds(pl.multiple_of(me * 16, 16), 16)
         for p in peers:
-            push(gsend.at[1, p, :, cols], tab_out.at[mine_rows, cols], p, 5).start()
-        pltpu.make_async_copy(gsend.at[1, me, :, cols], tab_out.at[mine_rows, cols], out_sem.at[0]).start()
+            push(gsend.at[1, p, :, cols], gnow_out.at[me, :, cols], p, 5).start()
+        pltpu.make_async_copy(gsend.at[1, me, :, cols], gnow_out.at[me, :, cols], out_sem.at[0]).start()
 
     lane128 = iota((CAP, 128), 1)
     rows = jnp.broadcast_to(gates_all[...], (N, 8, 512)).reshape(CAP, 512)
@@ -366,7 +365,7 @@
     pltpu.make_async_copy(dh_v, dh_out, out_sem.at[0]).start()
     pltpu.make_async_copy(da_v, da_out, out_sem.at[0]).start()
 
-    cp_dlog = pltpu.make_async_copy(dlog_v, tab_out.at[:, pl.ds(NOW * CH, 128)], out_sem.at[0])
+    cp_dlog = pltpu.make_async_copy(dlog_v, tab_out, out_sem.at[0])
     cp_dlog.start()
 
     gate_gather()
@@ -397,8 +396,7 @@
         cp.start()
     wait_recv(lossall, 7)
     loss_out[0, 0] = jnp.sum(lossall[...]) * scale
-    part = tab_out.at[pl.ds(0, (N - 1) * 16), pl.ds(0, NOW * CH)]
-    pltpu.make_async_copy(part, part, recv_sem.at[5]).wait()
+    wait_recv(gnow_out, 5)
 
     wait_send(selall, 0)
     wait_send(gates_all, 2)
@@ -408,7 +406,7 @@
     pltpu.make_async_copy(part, part, send_sem.at[1]).wait()
     for c in range(NOW):
         cols = pl.ds(c * CH, CH)
-        pltpu.make_async_copy(gsend.at[1, me, :, cols], tab_out.at[pl.ds(pl.multiple_of(me * 16, 16), 16), cols], out_sem.at[0]).wait()
+        pltpu.make_async_copy(gsend.at[1, me, :, cols], gnow_out.at[me, :, cols], out_sem.at[0]).wait()
     wait_send(rsend, 3)
     wait_send(lossall, 7)
     push(ggpart.at[1 - core], ggpair, twin, 8).wait_send()
@@ -434,11 +432,11 @@
     shape = jax.ShapeDtypeStruct
     return pl.pallas_call(
         functools.partial(comm_kernel, scale),
-        out_shape=[shape((N, 16, HID), BF), shape((TOK, NOW * CH + 128), BF), shape((N, 16, 2 * HID - NOW * CH), BF),
+        out_shape=[shape((N, 16, HID), BF), shape((N, 16, NOW * CH), BF), shape((N, 16, 2 * HID - NOW * CH), BF), shape((TOK, 128), BF),
                    shape((64, HID), F32), shape((1, 1), F32),
                    shape((LE, CAP, HID), BF), shape((LE, CAP, FF), BF), shape((LE, CAP, HID), BF), shape((LE, CAP, FF), BF)],
         in_specs=[vmem, any_, any_, any_, any_, any_],
-        out_specs=[any_, any_, any_, any_, pl.BlockSpec(memory_space=pltpu.SMEM), any_, any_, any_, any_],
+        out_specs=[any_, any_, any_, any_, any_, pl.BlockSpec(memory_space=pltpu.SMEM), any_, any_, any_, any_],
         scratch_shapes=[
             V((TOK, HID), BF), V((TOK, HID), BF), V((64, HID), BF),
             V((3, HID, FF), BF), V((3, FF, HID), BF),
@@ -539,7 +537,7 @@
     )(xl, da, u, dh, y, gg, loss)
 
 
-def gradx_kernel(scale, late_in, r_v, tab_v, gw_v, gx, late_v, gx_v, in_sem, out_sem):
+def gradx_kernel(scale, late_in, now_v, r_v, tab_v, gw_v, gx, late_v, gx_v, in_sem, out_sem):
     def pieces(c):
         cols = pl.ds(c * CH, CH)
         out = [pltpu.make_async_copy(late_in.at[:, :, cols], late_v.at[:, :, cols], in_sem.at[c])]
@@ -550,16 +548,16 @@
     for c in range(NCH):
         for cp in pieces(c):
             cp.start()
-    block = tab_v[0:16, NOW * CH:NOW * CH + 128]
+    block = tab_v[0:16, :]
     rows16 = dot(block, ones_where(iota((128, 512), 0) == 64 + iota((128, 512), 1) % 64))
     ids = jnp.sum(jnp.where(iota((16, 512), 1) // 64 == iota((16, 512), 0), rows16, 0.0), axis=0, keepdims=True)
     one = jnp.where(iota((TOK, 512), 0).astype(F32) == ids, 1.0, 0.0).astype(BF)
-    dlog = tab_v[:, NOW * CH:NOW * CH + 64]
+    dlog = tab_v[:, 0:64]
     for c in range(NCH):
         cols = pl.ds(c * CH, CH)
         tot = r_v[:, cols].astype(F32) * scale + dot(dlog, gw_v[:, cols])
         if c < NOW:
-            tot = tot + dot(one[:, 256:512], tab_v[:, cols])
+            tot = tot + dot(one[:, 256:512], now_v[:, :, cols].reshape(256, CH))
         for cp in pieces(c):
             cp.wait()
         if c >= NOW:
@@ -571,29 +569,29 @@
         pltpu.make_async_copy(gx_v.at[:, cols], gx.at[:, cols], out_sem).wait()
 
 
-def gradx_call(late, r, tab, gw, scale):
+def gradx_call(late, now, r, tab, gw, scale):
     any_ = pl.BlockSpec(memory_space=pl.ANY)
     vmem = pl.BlockSpec(memory_space=pltpu.VMEM)
     V = pltpu.VMEM
     return pl.pallas_call(
         functools.partial(gradx_kernel, scale),
-        in_specs=[any_, vmem, vmem, vmem],
+        in_specs=[any_, vmem, vmem, vmem, vmem],
         out_specs=any_,
         out_shape=jax.ShapeDtypeStruct((TOK, HID), BF),
         scratch_shapes=[V((N, 16, 2 * HID - NOW * CH), BF), V((TOK, HID), BF), pltpu.SemaphoreType.DMA((NCH,)), pltpu.SemaphoreType.DMA],
         compiler_params=pltpu.CompilerParams(vmem_limit_bytes=16000000),
         name='grad_x',
-    )(late, r, tab, gw)
+    )(late, now, r, tab, gw)
 
 
 def solution(mesh):
     def device_step(x, gate_w, up_w, down_w, expert_picks, loss_w):
         scale = 1.0 / math.sqrt(TOK * N * HID)
         gate_t = gate_w.T
-        y, tab, later, gg, loss, xl, u, dh, da = comm_call(expert_picks, x, gate_t, up_w, down_w, loss_w, scale)
+        y, now, later, tab, gg, loss, xl, u, dh, da = comm_call(expert_picks, x, gate_t, up_w, down_w, loss_w, scale)
         later = lax.all_to_all(later, 'ep', 0, 0, tiled=True)
         grad_up, grad_down, y, gg, loss = wgrad1_call(xl, da, u, dh, y, gg, loss)
-        grad_x = gradx_call(later, loss_w, tab, gate_t, scale)
+        grad_x = gradx_call(later, now, loss_w, tab, gate_t, scale)
         return y.reshape(TOK, HID), loss[0, 0], grad_x, grad_up, grad_down, gg.T
 
     return jax.shard_map(device_step, mesh=mesh,

time: 104 us -> 102 us (0.981)
  Pallas kernels: 98.7 us -> 95.5 us
    pallas_call x1, Pallas kernels: 76.7 us -> 73.6 us  [comm_call(): pl.pallas_call(functools.partial(comm_kernel, scale), out_shape=[shape((N...]
where the time goes in v3:
time: 102 us; the launch traced here: 101 us
  Pallas kernels  95.5 us (94%)
  starting transfers between devices  2.89 us (3%)
  waiting for transfers between devices  2.26 us (2%)
    pallas_call x1, Pallas kernels, comm_call(): pl.pallas_call(functools.partial(comm_kernel, scale), out_shape=[shape((N...  73.6 us
    pallas_call x1, Pallas kernels, wgrad1_call(): pl.pallas_call(wgrad1_kernel, in_specs=[any_] * 6 + [smem], out_specs=[an...  19.7 us
    all_to_all x1, starting transfers between devices, device_step(): later = lax.all_to_all(later, 'ep', 0, 0, tiled=True)  2.89 us
    pallas_call x1, Pallas kernels, gradx_call(): pl.pallas_call(functools.partial(gradx_kernel, scale), in_specs=[any_, vm...  2.29 us
    all_to_all x1, waiting for transfers between devices, device_step(): later = lax.all_to_all(later, 'ep', 0, 0, tiled=True)  2.26 us
  transfers between devices with their start and end apart: 1, of which 1 were waited for; matrix products, arithmetic and copies ran while one was open for 0% of the time, Pallas kernels for 19%

profile of v3, /device:TPU:0, one launch (start us, length us, event | category | flops | bytes accessed | tf_op | source)
XLA Modules:
  0.0 101.4 jit_solution(1436451057363286562)
XLA Ops:
  0.6 73.6 %exchange.1 = (bf16[16,16,2048]{2,1,0:T(8,128)(2,1)}, bf16[16,16,1024]{2,1,0:T(8,128)(2,1)}, bf16[16,16,3072]{2,1,0:T(8,128)(2,1)}, bf16[256,128]{1,0:T(8,128)(2...) custom-call(s32[4,128]{1,0:T(4,128)} %sel_ref.1, ...), custom_call_target="tpu_custom_call" | custom-call | tf_op jit(solution)/shard_map/exchange/pallas_call | solution.py:433
  74.2 2.9 %all-to-all-start = ((bf16[16,16,3072]{2,1,0:T(8,128)(2,1)}), bf16[16,16,3072]{2,1,0:T(8,128)(2,1)S(1)}, u32[]{:S(2)}, u32[]{:S(2)}) async-start(bf16[16,16,3072]{2,1,0:T(8,128)(2,1)} %get-tuple-element.30), calls=%async_computation | async-start | bytes 3145728 | tf_op jit(solution)/shard_map/all_to_all | solution.py:592
  77.1 0.0 copy-start
  77.1 0.0 copy-start.1
  77.1 0.0 copy-start.2
  77.1 0.0 copy-start.3
  77.1 19.7 %weight_grads_a.1 = (bf16[4,2048,1408]{2,1,0:T(8,128)(2,1)}, bf16[4,1408,2048]{2,1,0:T(8,128)(2,1)}, bf16[16,16,2048]{2,1,0:T(8,128)(2,1)}, f32[64,2048]{1,0:T(8,128)}, f32[1,1]{1,0:T(1,128)}) custom-call(bf16[4,128,2048]{2,1,0:T(8,128)(2,1)} %get-tuple-element.21.xl_in, bf16[4,128,1408]{2,1,0:T(8,128)(2,1)} %get-tuple-element.22.da_in, ...), custom_call_target="tpu_custom_call" | custom-call | flops 5905580032 | bytes 50331648 | tf_op jit(solution)/shard_map/weight_grads_a/pallas_call | solution.py:526
  96.8 2.3 %all-to-all-done.late_in = bf16[16,16,3072]{2,1,0:T(8,128)(2,1)S(1)} async-done(((bf16[16,16,3072]{2,1,0:T(8,128)(2,1)}), bf16[16,16,3072]{2,1,0:T(8,128)(2,1)S(1)}, u32[]{:S(2)}, u32[]{:S(2)}) %all-to-all-start) | async-done | bytes 1572896 | tf_op jit(solution)/shard_map/all_to_all | solution.py:592
  99.1 0.0 copy-done
  99.1 0.0 copy-done.1
  99.1 0.0 copy-done.2
  99.1 0.0 copy-done.3
  99.1 2.3 %grad_x.1 = bf16[256,2048]{1,0:T(8,128)(2,1)} custom-call(bf16[16,16,3072]{2,1,0:T(8,128)(2,1)S(1)} %all-to-all-done.late_in, bf16[16,16,1024]{2,1,0:T(8,128)(2,1)S(1)} %copy-done.2, bf16[256,2048]{1,0:T(8,128)(2,1)S(1)} %copy-done, bf16[256,128]{1,0:T(8,128)(2,1)S(1)} %copy-done.3, bf16[64,2048]{1,0:T(8,128)(2,1)S(1)} %bitcast.5), custom_call_target="tpu_custom_call" | custom-call | tf_op jit(solution)/shard_map/grad_x/pallas_call | solution.py:576
Async XLA Ops:
  74.2 24.9 %all-to-all-start = ((bf16[16,16,3072]{2,1,0:T(8,128)(2,1)}), bf16[16,16,3072]{2,1,0:T(8,128)(2,1)S(1)}, u32[]{:S(2)}, u32[]{:S(2)}) async-start(bf16[16,16,3072]{2,1,0:T(8,128)(2,1)} %get-tuple-element.30), calls=%async_computation | async-start | bytes 3145728 | tf_op jit(solution)/shard_map/all_to_all | solution.py:592
  77.1 22.0 %copy-start = (bf16[256,2048]{1,0:T(8,128)(2,1)S(1)}, bf16[256,2048]{1,0:T(8,128)(2,1)}, u32[]{:S(2)}) copy-start(bf16[256,2048]{1,0:T(8,128)(2,1)} %r_v.1) | copy-start | bytes 3145732
  77.1 22.0 %copy-start.1 = (bf16[2048,64]{0,1:T(8,128)(2,1)S(1)}, bf16[2048,64]{0,1:T(8,128)(2,1)}, u32[]{:S(2)}) copy-start(bf16[2048,64]{0,1:T(8,128)(2,1)} %param.7) | copy-start | bytes 786436
  77.1 22.0 %copy-start.2 = (bf16[16,16,1024]{2,1,0:T(8,128)(2,1)S(1)}, bf16[16,16,1024]{2,1,0:T(8,128)(2,1)}, u32[]{:S(2)}) copy-start(bf16[16,16,1024]{2,1,0:T(8,128)(2,1)} %get-tuple-element.31.now_v) | copy-start | bytes 1572868
  77.1 22.0 %copy-start.3 = (bf16[256,128]{1,0:T(8,128)(2,1)S(1)}, bf16[256,128]{1,0:T(8,128)(2,1)}, u32[]{:S(2)}) copy-start(bf16[256,128]{1,0:T(8,128)(2,1)} %get-tuple-element.32.tab_v) | copy-start | bytes 196612
